TPU v7x, 32 devices: a whole 2x2x4 slice. The times are simulated.
32 devices in a mesh: gx: 4 (over z), gy: 8 (over y, x, core).
Axes of the slice: x: 2, y: 2, z: 4, core: 2. Of those that a mesh axis runs over, the one named last changes fastest.
Arguments:
- rhs: float32 [4, 8, 1, 3, 200, 128], P('gx', 'gy'), may hold values from -25 to 25
- stiff_inverse: bfloat16 [4, 8, 1, 1200, 1200], P('gx', 'gy'), may hold values from -2 to 6, as said below
- schur: bfloat16 [4, 8, 1, 1200, 1200], P('gx', 'gy'), may hold values from -2 to 6, as said below
- phi: bfloat16 [4, 8, 1, 24, 1200], P('gx', 'gy'), may hold values from -0.1875 to 0.1875
- coarse_inverse: float32 [192, 192], P(('gx', 'gy')), may hold values from -2 to 6, as said below
- incidence: int32 [4, 8, 1, 8], P('gx', 'gy'), may hold values from 0 to 63, as said below
- pairing: int32 [4, 8, 1, 3, 200], P('gx', 'gy'), may hold values from 0 to 199, as said below
Outputs:
- multipliers: float32 [4, 8, 1, 3, 200, 128], P('gx', 'gy')
- reduction: float32 [128], replicated
Inputs may be any that keep to these rules, and one draw needn't show every extreme that they name: `stiff_inverse`: each block is symmetric positive definite. `schur`: each block is symmetric positive definite. `coarse_inverse`: symmetric positive definite. `incidence`: the corners of the subdomain grid, periodic in the first two dimensions, under an arbitrary numbering of the 64 nodes: corner c of subdomain (x, y, z) is the grid point (x + c % 2, y + (c // 2) % 2, z + c // 4), and subdomains that share a grid point name the same node. `pairing`: each row over the last dimension is a permutation of 0 to 199.
All inputs are finite; a program needn't handle non-finite values.
Results may differ from a plain program's by a relative error of at most 0.0027.
Values sent between devices are 32-bit elements; how exact they have to be, the bound alone decides.
A program may use at most 64 MiB of HBM per device.

v0:
```python
import jax
import jax.numpy as jnp
from jax import lax
from jax.sharding import PartitionSpec as P

ITERS = 2
largest_index = lax.Precision.HIGHEST


def passed_along(array, axis, by):
    peers = lax.axis_size(axis)
    return lax.ppermute(array, axis, [(i, (i + by) % peers) for i in range(peers)])


def local(rhs, stiff_inverse, schur, phi, coarse_inverse, incidence, pairing):
    blocks = rhs.shape[2]
    face_dofs = rhs.shape[4]
    load_cases = rhs.shape[5]
    interface = 6 * face_dofs
    stiffness = stiff_inverse[0, 0]
    schur_block_stack = schur[0, 0]
    coupling_matrix = phi[0, 0].astype(jnp.float32)
    local_ids = incidence[0, 0]
    level = jnp.arange(blocks)[:, None]
    axis_id = jnp.arange(3)[None, :]
    active = jnp.where((level == blocks - 1) & (axis_id == 2), 0.0, 1.0).astype(jnp.float32)[
        :, :, None, None
    ]
    perm_table = (pairing[0, 0][..., None] == jnp.arange(face_dofs)[None, None, None, :]).astype(
        jnp.float32
    )
    owner_weights = None
    own_ids = jnp.concatenate([local_ids[:, 0], local_ids[-1:, 4]])
    own_dofs = (3 * own_ids[:, None] + jnp.arange(3, dtype=jnp.int32)[None, :]).reshape(-1)
    picked = jnp.take(
        lax.all_gather(coarse_inverse, ("gx", "gy"), axis=0, tiled=True), own_dofs, axis=1
    )
    every_owner = lax.all_gather(own_ids, ("gx", "gy"), axis=0, tiled=True)
    gathered_dofs = (3 * every_owner[:, None] + jnp.arange(3, dtype=jnp.int32)[None, :]).reshape(-1)
    owner_weights = jnp.take(picked, gathered_dofs, axis=0)

    def transpose_jump(values):
        masked = values * active
        moved = jnp.einsum("sakj,sakr->sajr", perm_table, masked, precision=largest_index)
        lower_x = passed_along(moved[:, 0], "gx", 1)
        lower_y = passed_along(moved[:, 1], "gy", 1)
        lower_z = jnp.concatenate([jnp.zeros_like(moved[:1, 2]), moved[:-1, 2]], axis=0)
        return jnp.stack(
            [-lower_x, masked[:, 0], -lower_y, masked[:, 1], -lower_z, masked[:, 2]], axis=1
        )

    def jump_field(field):
        upper_x = passed_along(field[:, 0], "gx", -1)
        upper_y = passed_along(field[:, 2], "gy", -1)
        upper_z = jnp.concatenate([field[1:, 4], jnp.zeros_like(field[:1, 4])], axis=0)
        neighbour = jnp.stack([upper_x, upper_y, upper_z], axis=1)
        paired = jnp.einsum("sakj,sajr->sakr", perm_table, neighbour, precision=largest_index)
        higher = jnp.stack([field[:, 1], field[:, 3], field[:, 5]], axis=1)
        return (higher - paired) * active

    def apply_local(matrices, field):
        low_field = field.reshape(blocks, interface, load_cases).astype(jnp.bfloat16)
        result = jnp.einsum("snm,smr->snr", matrices, low_field, preferred_element_type=jnp.float32)
        return result.reshape(blocks, 6, face_dofs, load_cases)

    def precondition(values):
        field = 0.5 * transpose_jump(values)
        return 0.5 * jump_field(apply_local(schur_block_stack, field))

    def inner_product(left, right):
        return jnp.sum(left * right, axis=(0, 1, 2))

    def energy_total(partial_value):
        return lax.psum(partial_value, ("gx", "gy"))

    residual = rhs[0, 0] * active
    multipliers = jnp.zeros_like(residual)
    preconditioned = precondition(residual)
    partial_energy = inner_product(residual, preconditioned)
    energy = energy_total(partial_energy)
    direction_field = None
    search_corner_values = None
    start_energy = energy
    direction = preconditioned
    for iteration in range(ITERS):
        direction_field = transpose_jump(direction)
        split = jnp.einsum(
            "vzh,vhq->vzq",
            coupling_matrix,
            direction_field.reshape(blocks, interface, load_cases),
            precision=largest_index,
        ).reshape(blocks, 2, 2, 2, 3, load_cases)
        empty = jnp.zeros((1, 2, 2, 3, load_cases), jnp.float32)
        by_node = jnp.concatenate([split[:, 0], empty], axis=0) + jnp.concatenate(
            [empty, split[:, 1]], axis=0
        )
        from_x = passed_along(by_node[:, :, 1], "gx", 1)
        along_x = by_node[:, :, 0] + from_x
        from_y = passed_along(along_x[:, 1], "gy", 1)
        owned = (along_x[:, 0] + from_y).reshape(-1, load_cases)
        gathered = lax.all_gather(owned, ("gx", "gy"), axis=0, tiled=True)
        solved = jnp.dot(owner_weights.T, gathered, precision=largest_index).reshape(
            blocks + 1, 3, load_cases
        )
        from_upper_x = passed_along(solved, "gx", -1)
        pair = jnp.stack([solved, from_upper_x], axis=0)
        from_upper_y = passed_along(pair, "gy", -1)
        quad = jnp.stack([pair, from_upper_y], axis=0)
        neighbour_values = jnp.stack([quad[:, :, :blocks], quad[:, :, 1:]], axis=0)
        neighbour_values = jnp.transpose(neighbour_values, (3, 0, 1, 2, 4, 5)).reshape(
            blocks, -1, load_cases
        )
        search_corner_values = neighbour_values
        spread_operator = jnp.einsum(
            "xgy,xgh->xyh", coupling_matrix, search_corner_values, precision=largest_index
        )
        displacement = apply_local(stiffness, direction_field) + spread_operator.reshape(
            blocks, 6, face_dofs, load_cases
        )
        product_field = jump_field(displacement)
        curvature = lax.psum(inner_product(direction, product_field), ("gx", "gy"))
        alpha = energy / curvature
        multipliers = multipliers + alpha * direction
        residual = residual - alpha * product_field
        preconditioned = precondition(residual)
        partial_energy = inner_product(residual, preconditioned)
        if iteration + 1 < ITERS:
            energy_next = energy_total(partial_energy)
            ratio = energy_next / energy
            direction = preconditioned + ratio * direction
        else:
            energy_next = energy_total(partial_energy)
        energy = energy_next
    return (multipliers[None, None], energy / start_energy)


def solution(mesh):
    return jax.shard_map(
        local,
        mesh=mesh,
        in_specs=(
            P("gx", "gy", None, None, None, None),
            P("gx", "gy", None, None, None),
            P("gx", "gy", None, None, None),
            P("gx", "gy", None, None, None),
            P(("gx", "gy"), None),
            P("gx", "gy", None, None),
            P("gx", "gy", None, None, None),
        ),
        out_specs=(P("gx", "gy", None, None, None, None), P()),
        check_vma=False,
    )
```

profile of v0, /device:TPU:0, one launch (start us, length us, event | category | flops | bytes accessed | tf_op | source)
XLA Modules:
  0.0 463.3 jit_solution(669811901619081959)
XLA Ops:
  1.5 1.9 convolution_bitcast_fusion.4
  4.6 2.6 collective-permute-start
  7.1 1.4 fusion.99
  10.1 1.8 fusion.32
  11.9 1.4 fusion.96
  13.3 40.4 %all-reduce.4 = s32[64]{0:T(128)S(1)} all-reduce(s32[64]{0:T(128)S(1)} %fusion.96), channel_id=1, replica_groups=mesh['gx'=4,'gy'=8] {'gx','gy'}, use_global_device_ids=true, to_apply=%add.4 | all-reduce | flops 64 | bytes 512
  53.9 41.3 %all-gather = f32[32,6,192]{2,1,0:T(8,128)S(1)} all-gather(f32[1,6,192]{2,1,0:T(8,128)} %bitcast.317), channel_id=1, replica_groups=mesh['gx'=4,'gy'=8] {'gx','gy'}, dimensions={0}, use_global_device_ids=true | all-gather | bytes 152064 | tf_op jit(solution)/shard_map/all_gather | solution.py:36
  103.6 2.8 fusion
  106.6 5.0 %collective-permute-done.2 = f32[1,200,128]{2,1,0:T(8,128)S(1)} collective-permute-done((f32[1,200,128]{2,1,0:T(8,128)S(1)}, f32[1,200,128]{2,1,0:T(8,128)S(1)}, u32[]{:S(2)}, u32[]{:S(2)}) %collective-permute-start.2) | collective-permute-done | bytes 102432 | tf_op jit(solution)/shard_map/ppermute | solution.py:12
  114.1 5.6 %collective-permute-done.4 = f32[1,200,128]{2,1,0:T(8,128)S(1)} collective-permute-done((f32[1,200,128]{2,1,0:T(8,128)S(1)}, f32[1,200,128]{2,1,0:T(8,128)S(1)}, u32[]{:S(2)}, u32[]{:S(2)}) %collective-permute-start.4) | collective-permute-done | bytes 102432 | tf_op jit(solution)/shard_map/ppermute | solution.py:12
  121.6 4.9 %collective-permute-done.6 = f32[2,2,3,128]{3,2,1,0:T(4,128)S(1)} collective-permute-done((f32[2,2,3,128]{3,2,1,0:T(4,128)S(1)}, f32[2,2,3,128]{3,2,1,0:T(4,128)S(1)}, u32[]{:S(2)}, u32[]{:S(2)}) %collective-permute-start.6) | collective-permute-done | bytes 6176 | tf_op jit(solution)/shard_map/ppermute | solution.py:12
  129.2 2.1 collective-permute-done.7
  132.0 39.4 %all-gather.1 = f32[32,6,128]{2,1,0:T(8,128)} all-gather(f32[1,6,128]{2,1,0:T(8,128)S(1)} %reshape.812), channel_id=1, replica_groups=mesh['gx'=4,'gy'=8] {'gx','gy'}, dimensions={0}, use_global_device_ids=true | all-gather | bytes 101376 | tf_op jit(solution)/shard_map/all_gather | solution.py:101
  173.6 3.6 collective-permute-done.8
  177.9 1.9 convert_element_type.109
  182.4 2.0 fusion.7
  184.4 3.2 collective-permute-start.10
  187.5 2.0 collective-permute-start.11
  190.2 1.6 collective-permute-done.11
  193.0 38.4 %all-reduce.5 = (f32[128]{0:T(128)S(1)}, f32[128]{0:T(128)S(1)}) all-reduce(f32[128]{0:T(128)S(1)} %get-tuple-element.3, f32[128]{0:T(128)S(1)} %get-tuple-element.2), channel_id=1, replica_groups=mesh['gx'=4,'gy'=8] {'gx','gy'}, use_global_device_ids=true, to_apply=%region_1.2 | all-reduce | flops 256 | bytes 2048 | tf_op jit(solution)/shard_map/psum | solution.py:74
  232.0 1.5 multiply_bitcast_fusion.2
  234.4 2.2 collective-permute-start.12
  236.6 4.3 collective-permute-done.12
  242.7 1.7 collective-permute-start.14
  244.5 3.0 collective-permute-done.14
  247.5 1.8 multiply_reduce_fusion.1
  249.3 39.4 %psum.37 = f32[128]{0:T(128)S(1)} all-reduce(f32[128]{0:T(128)} %get-tuple-element.65), channel_id=1, replica_groups=mesh['gx'=4,'gy'=8] {'gx','gy'}, use_global_device_ids=true, to_apply=%region_5.6 | all-reduce | flops 128 | bytes 1024 | tf_op jit(solution)/shard_map/psum | solution.py:74
  290.7 2.1 collective-permute-start.16
  292.7 4.5 collective-permute-done.16
  299.0 1.4 collective-permute-start.18
  300.4 4.1 collective-permute-done.18
  304.5 3.9 collective-permute-done.19
  308.4 40.7 %all-gather.2 = f32[32,6,128]{2,1,0:T(8,128)} all-gather(f32[1,6,128]{2,1,0:T(8,128)S(1)} %reshape.814), channel_id=1, replica_groups=mesh['gx'=4,'gy'=8] {'gx','gy'}, dimensions={0}, use_global_device_ids=true | all-gather | bytes 101376 | tf_op jit(solution)/shard_map/all_gather | solution.py:101
  349.1 1.5 reshape.815
  352.0 3.6 collective-permute-done.20
  355.6 1.8 convert_element_type.113
  357.5 1.4 fusion.64
  358.9 1.9 fusion.6
  360.9 1.9 collective-permute-start.22
  362.8 1.8 collective-permute-start.23
  364.6 1.6 collective-permute-done.22
  368.1 38.5 %psum.38 = f32[128]{0:T(128)S(1)} all-reduce(f32[128]{0:T(128)S(1)} %get-tuple-element.67), channel_id=1, replica_groups=mesh['gx'=4,'gy'=8] {'gx','gy'}, use_global_device_ids=true, to_apply=%region_7.8 | all-reduce | flops 128 | bytes 1024 | tf_op jit(solution)/shard_map/psum | solution.py:121
  406.6 2.1 multiply_bitcast_fusion
  409.6 2.2 collective-permute-start.24
  411.8 4.3 collective-permute-done.24
  417.9 1.8 collective-permute-start.26
  419.7 3.0 collective-permute-done.26
  423.2 39.6 %psum.39 = f32[128]{0:T(128)S(1)} all-reduce(f32[128]{0:T(128)S(1)} %fusion.16), channel_id=1, replica_groups=mesh['gx'=4,'gy'=8] {'gx','gy'}, use_global_device_ids=true, to_apply=%region_9.10 | all-reduce | flops 128 | bytes 1024 | tf_op jit(solution)/shard_map/psum | solution.py:74
  (199 shorter events, 41.4 us)
Async XLA Ops:
  0.6 181.7 %copy-start = (bf16[1,1,1,1200,1200]{4,3,2,1,0:T(8,128)(2,1)S(1)}, bf16[1,1,1,1200,1200]{4,3,2,1,0:T(8,128)(2,1)}, u32[]{:S(2)}) copy-start(bf16[1,1,1,1200,1200]{4,3,2,1,0:T(8,128)(2,1)} %param.8) | copy-start | bytes 8640004
  0.7 111.0 %copy-start.12 = (f32[3]{0:T(128)}, f32[3]{0:T(128)S(1)}, u32[]{:S(2)}) copy-start(f32[3]{0:T(128)S(1)} %compare_select_fusion.4) | copy-start | bytes 40
  4.1 96.7 %collective-permute-start.1 = (f32[1,200,128]{2,1,0:T(8,128)S(1)}, f32[1,200,128]{2,1,0:T(8,128)}, u32[]{:S(2)}, u32[]{:S(2)}) collective-permute-start(f32[1,200,128]{2,1,0:T(8,128)S(1)} %get-tuple-element.47), channel_id=1, source_target_pairs={{0,1},{1,2},{2,3},{3,4},{4,5},{5,6},{6,7},{7,0},{8,9},{9,10},{10,1... | collective-permute-start | bytes 307208 | tf_op jit(solution)/shard_map/ppermute | solution.py:12
  4.6 94.4 %collective-permute-start = (f32[1,200,128]{2,1,0:T(8,128)}, f32[1,200,128]{2,1,0:T(8,128)}, u32[]{:S(2)}, u32[]{:S(2)}) collective-permute-start(f32[1,200,128]{2,1,0:T(8,128)} %get-tuple-element.48), channel_id=1, source_target_pairs={{0,8},{8,16},{16,24},{24,0},{1,9},{9,17},{17,25},{25,1},{2,10},{10... | collective-permute-start | bytes 307208 | tf_op jit(solution)/shard_map/ppermute | solution.py:12
  99.0 12.7 %copy-start.20 = (f32[3]{0:T(128)}, f32[3]{0:T(128)S(1)}, u32[]{:S(2)}) copy-start(f32[3]{0:T(128)S(1)} %pad.44.clone) | copy-start | bytes 40
  106.4 14.1 %copy-start.11 = (bf16[1,1,1,24,1200]{4,3,2,1,0:T(8,128)(2,1)S(1)}, bf16[1,1,1,24,1200]{4,3,2,1,0:T(8,128)(2,1)}, u32[]{:S(2)}) copy-start(bf16[1,1,1,24,1200]{4,3,2,1,0:T(8,128)(2,1)} %param.10) | copy-start | bytes 172804
  106.4 20.6 %copy-start.16 = (s32[192,1]{0,1:T(1,128)S(1)}, s32[192,1]{0,1:T(1,128)}, u32[]{:S(2)}) copy-start(s32[192,1]{0,1:T(1,128)} %compare_select_fusion) | copy-start | bytes 2308
  106.5 5.2 %collective-permute-start.2 = (f32[1,200,128]{2,1,0:T(8,128)S(1)}, f32[1,200,128]{2,1,0:T(8,128)S(1)}, u32[]{:S(2)}, u32[]{:S(2)}) collective-permute-start(f32[1,200,128]{2,1,0:T(8,128)S(1)} %get-tuple-element.34), channel_id=1, source_target_pairs={{0,24},{8,0},{16,8},{24,16},{1,25},{9,1},{17,9},{25,17},{2,26},{10... | collective-permute-start | bytes 307208 | tf_op jit(solution)/shard_map/ppermute | solution.py:12
  106.6 5.1 %collective-permute-start.3 = (f32[1,200,128]{2,1,0:T(8,128)S(1)}, f32[1,200,128]{2,1,0:T(8,128)S(1)}, u32[]{:S(2)}, u32[]{:S(2)}) collective-permute-start(f32[1,200,128]{2,1,0:T(8,128)S(1)} %get-tuple-element.35), channel_id=1, source_target_pairs={{0,7},{1,0},{2,1},{3,2},{4,3},{5,4},{6,5},{7,6},{8,15},{9,8},{10,9... | collective-permute-start | bytes 307208 | tf_op jit(solution)/shard_map/ppermute | solution.py:12
  113.1 6.5 %collective-permute-start.4 = (f32[1,200,128]{2,1,0:T(8,128)S(1)}, f32[1,200,128]{2,1,0:T(8,128)S(1)}, u32[]{:S(2)}, u32[]{:S(2)}) collective-permute-start(f32[1,200,128]{2,1,0:T(8,128)S(1)} %get-tuple-element.46), channel_id=1, source_target_pairs={{0,8},{8,16},{16,24},{24,0},{1,9},{9,17},{17,25},{25,1},{2,10},{10... | collective-permute-start | bytes 307208 | tf_op jit(solution)/shard_map/ppermute | solution.py:12
  113.3 6.4 %collective-permute-start.5 = (f32[1,200,128]{2,1,0:T(8,128)S(1)}, f32[1,200,128]{2,1,0:T(8,128)S(1)}, u32[]{:S(2)}, u32[]{:S(2)}) collective-permute-start(f32[1,200,128]{2,1,0:T(8,128)S(1)} %get-tuple-element.45), channel_id=1, source_target_pairs={{0,1},{1,2},{2,3},{3,4},{4,5},{5,6},{6,7},{7,0},{8,9},{9,10},{10,1... | collective-permute-start | bytes 307208 | tf_op jit(solution)/shard_map/ppermute | solution.py:12
  120.9 5.5 %collective-permute-start.6 = (f32[2,2,3,128]{3,2,1,0:T(4,128)S(1)}, f32[2,2,3,128]{3,2,1,0:T(4,128)S(1)}, u32[]{:S(2)}, u32[]{:S(2)}) collective-permute-start(f32[2,2,3,128]{3,2,1,0:T(4,128)S(1)} %fusion.85), channel_id=1, source_target_pairs={{0,8},{8,16},{16,24},{24,0},{1,9},{9,17},{17,25},{25,1},{2,10},{10... | collective-permute-start | bytes 18440 | tf_op jit(solution)/shard_map/ppermute | solution.py:12
  127.0 4.2 collective-permute-start.7
  173.5 3.7 collective-permute-start.8
  177.8 2.0 collective-permute-start.9
  181.8 9.9 %copy-start.5 = (f32[1,1,1,3,200,128]{5,4,3,2,1,0:T(8,128)S(1)}, f32[1,1,1,3,200,128]{5,4,3,2,1,0:T(8,128)}, u32[]{:S(2)}) copy-start(f32[1,1,1,3,200,128]{5,4,3,2,1,0:T(8,128)} %param.7) | copy-start | bytes 921604
  181.8 9.9 %copy-start.13 = (f32[3]{0:T(128)S(1)}, f32[3]{0:T(128)}, u32[]{:S(2)}) copy-start(f32[3]{0:T(128)} %copy-done.12) | copy-start | bytes 40
  181.8 9.9 %copy-start.21 = (f32[3]{0:T(128)S(1)}, f32[3]{0:T(128)}, u32[]{:S(2)}) copy-start(f32[3]{0:T(128)} %copy-done.20) | copy-start | bytes 40
  182.3 49.7 %copy-start.14 = (f32[3]{0:T(128)S(1)}, f32[3]{0:T(128)}, u32[]{:S(2)}) copy-start(f32[3]{0:T(128)} %copy-done.12) | copy-start | bytes 40
  184.4 5.8 %collective-permute-start.10 = (f32[1,200,128]{2,1,0:T(8,128)S(1)}, f32[1,200,128]{2,1,0:T(8,128)S(1)}, u32[]{:S(2)}, u32[]{:S(2)}) collective-permute-start(f32[1,200,128]{2,1,0:T(8,128)S(1)} %get-tuple-element.29), channel_id=1, source_target_pairs={{0,24},{8,0},{16,8},{24,16},{1,25},{9,1},{17,9},{25,17},{2,26},{10... | collective-permute-start | bytes 307208 | tf_op jit(solution)/shard_map/ppermute | solution.py:12
  187.5 4.2 collective-permute-start.11
  231.4 57.3 %copy-start.18 = (f32[128]{0:T(128)}, f32[128]{0:T(128)S(1)}, u32[]{:S(2)}) copy-start(f32[128]{0:T(128)S(1)} %get-tuple-element.4) | copy-start | bytes 1540
  231.4 10.3 %copy-start.1 = (bf16[1,1,1,1200,1200]{4,3,2,1,0:T(8,128)(2,1)S(1)}, bf16[1,1,1,1200,1200]{4,3,2,1,0:T(8,128)(2,1)}, u32[]{:S(2)}) copy-start(bf16[1,1,1,1200,1200]{4,3,2,1,0:T(8,128)(2,1)} %param.9) | copy-start | bytes 8640004
  233.5 14.0 %copy-start.6 = (f32[3,200,128]{2,1,0:T(8,128)}, f32[3,200,128]{2,1,0:T(8,128)S(1)}, u32[]{:S(2)}) copy-start(f32[3,200,128]{2,1,0:T(8,128)S(1)} %get-tuple-element.13) | copy-start | bytes 921604
  234.4 6.5 %collective-permute-start.12 = (f32[1,200,128]{2,1,0:T(8,128)S(1)}, f32[1,200,128]{2,1,0:T(8,128)S(1)}, u32[]{:S(2)}, u32[]{:S(2)}) collective-permute-start(f32[1,200,128]{2,1,0:T(8,128)S(1)} %get-tuple-element.44), channel_id=1, source_target_pairs={{0,8},{8,16},{16,24},{24,0},{1,9},{9,17},{17,25},{25,1},{2,10},{10... | collective-permute-start | bytes 307208 | tf_op jit(solution)/shard_map/ppermute | solution.py:12
  236.6 5.0 %collective-permute-start.13 = (f32[1,200,128]{2,1,0:T(8,128)S(1)}, f32[1,200,128]{2,1,0:T(8,128)S(1)}, u32[]{:S(2)}, u32[]{:S(2)}) collective-permute-start(f32[1,200,128]{2,1,0:T(8,128)S(1)} %get-tuple-element.43), channel_id=1, source_target_pairs={{0,1},{1,2},{2,3},{3,4},{4,5},{5,6},{6,7},{7,0},{8,9},{9,10},{10,1... | collective-permute-start | bytes 307208 | tf_op jit(solution)/shard_map/ppermute | solution.py:12
  242.7 107.9 %copy-start.9 = (f32[192,6]{1,0:T(8,128)S(1)}, f32[192,6]{1,0:T(8,128)}, u32[]{:S(2)}) copy-start(f32[192,6]{1,0:T(8,128)} %gather_fusion.1) | copy-start | bytes 13828
  242.7 4.7 %collective-permute-start.14 = (f32[1,200,128]{2,1,0:T(8,128)S(1)}, f32[1,200,128]{2,1,0:T(8,128)S(1)}, u32[]{:S(2)}, u32[]{:S(2)}) collective-permute-start(f32[1,200,128]{2,1,0:T(8,128)S(1)} %get-tuple-element.24), channel_id=1, source_target_pairs={{0,24},{8,0},{16,8},{24,16},{1,25},{9,1},{17,9},{25,17},{2,26},{10... | collective-permute-start | bytes 307208 | tf_op jit(solution)/shard_map/ppermute | solution.py:12
  244.5 3.0 collective-permute-start.15
  290.7 6.5 %collective-permute-start.16 = (f32[1,200,128]{2,1,0:T(8,128)S(1)}, f32[1,200,128]{2,1,0:T(8,128)S(1)}, u32[]{:S(2)}, u32[]{:S(2)}) collective-permute-start(f32[1,200,128]{2,1,0:T(8,128)S(1)} %get-tuple-element.42), channel_id=1, source_target_pairs={{0,8},{8,16},{16,24},{24,0},{1,9},{9,17},{17,25},{25,1},{2,10},{10... | collective-permute-start | bytes 307208 | tf_op jit(solution)/shard_map/ppermute | solution.py:12
  292.7 5.0 %collective-permute-start.17 = (f32[1,200,128]{2,1,0:T(8,128)S(1)}, f32[1,200,128]{2,1,0:T(8,128)S(1)}, u32[]{:S(2)}, u32[]{:S(2)}) collective-permute-start(f32[1,200,128]{2,1,0:T(8,128)S(1)} %get-tuple-element.41), channel_id=1, source_target_pairs={{0,1},{1,2},{2,3},{3,4},{4,5},{5,6},{6,7},{7,0},{8,9},{9,10},{10,1... | collective-permute-start | bytes 307208 | tf_op jit(solution)/shard_map/ppermute | solution.py:12
  299.0 5.5 %collective-permute-start.18 = (f32[2,2,3,128]{3,2,1,0:T(4,128)S(1)}, f32[2,2,3,128]{3,2,1,0:T(4,128)S(1)}, u32[]{:S(2)}, u32[]{:S(2)}) collective-permute-start(f32[2,2,3,128]{3,2,1,0:T(4,128)S(1)} %fusion.83), channel_id=1, source_target_pairs={{0,8},{8,16},{16,24},{24,0},{1,9},{9,17},{17,25},{25,1},{2,10},{10... | collective-permute-start | bytes 18440 | tf_op jit(solution)/shard_map/ppermute | solution.py:12
  304.5 3.9 collective-permute-start.19
  351.9 3.7 collective-permute-start.20
  355.6 1.8 collective-permute-start.21
  357.5 9.4 %copy-start.8 = (f32[3,200,128]{2,1,0:T(8,128)S(1)}, f32[3,200,128]{2,1,0:T(8,128)}, u32[]{:S(2)}) copy-start(f32[3,200,128]{2,1,0:T(8,128)} %copy-done.7) | copy-start | bytes 921604
  357.5 9.4 %copy-start.15 = (f32[3]{0:T(128)S(1)}, f32[3]{0:T(128)}, u32[]{:S(2)}) copy-start(f32[3]{0:T(128)} %copy-done.12) | copy-start | bytes 40
  357.5 9.4 %copy-start.23 = (f32[3]{0:T(128)S(1)}, f32[3]{0:T(128)}, u32[]{:S(2)}) copy-start(f32[3]{0:T(128)} %copy-done.20) | copy-start | bytes 40
  358.9 47.7 %copy-start.25 = (f32[128]{0:T(128)S(1)}, f32[128]{0:T(128)}, u32[]{:S(2)}) copy-start(f32[128]{0:T(128)} %copy-done.24) | copy-start | bytes 1540
  358.9 47.7 %copy-start.17 = (f32[128]{0:T(128)S(1)}, f32[128]{0:T(128)}, u32[]{:S(2)}) copy-start(f32[128]{0:T(128)} %get-tuple-element.8) | copy-start | bytes 1540
  360.9 5.3 %collective-permute-start.22 = (f32[1,200,128]{2,1,0:T(8,128)S(1)}, f32[1,200,128]{2,1,0:T(8,128)S(1)}, u32[]{:S(2)}, u32[]{:S(2)}) collective-permute-start(f32[1,200,128]{2,1,0:T(8,128)S(1)} %get-tuple-element.19), channel_id=1, source_target_pairs={{0,24},{8,0},{16,8},{24,16},{1,25},{9,1},{17,9},{25,17},{2,26},{10... | collective-permute-start | bytes 307208 | tf_op jit(solution)/shard_map/ppermute | solution.py:12
  362.8 4.1 collective-permute-start.23
  406.6 10.3 %copy-start.2 = (bf16[1,1,1,1200,1200]{4,3,2,1,0:T(8,128)(2,1)S(1)}, bf16[1,1,1,1200,1200]{4,3,2,1,0:T(8,128)(2,1)}, u32[]{:S(2)}) copy-start(bf16[1,1,1,1200,1200]{4,3,2,1,0:T(8,128)(2,1)} %param.9) | copy-start | bytes 8640004
  409.6 6.5 %collective-permute-start.24 = (f32[1,200,128]{2,1,0:T(8,128)S(1)}, f32[1,200,128]{2,1,0:T(8,128)S(1)}, u32[]{:S(2)}, u32[]{:S(2)}) collective-permute-start(f32[1,200,128]{2,1,0:T(8,128)S(1)} %get-tuple-element.40), channel_id=1, source_target_pairs={{0,8},{8,16},{16,24},{24,0},{1,9},{9,17},{17,25},{25,1},{2,10},{10... | collective-permute-start | bytes 307208 | tf_op jit(solution)/shard_map/ppermute | solution.py:12
  411.8 5.0 %collective-permute-start.25 = (f32[1,200,128]{2,1,0:T(8,128)S(1)}, f32[1,200,128]{2,1,0:T(8,128)S(1)}, u32[]{:S(2)}, u32[]{:S(2)}) collective-permute-start(f32[1,200,128]{2,1,0:T(8,128)S(1)} %get-tuple-element.39), channel_id=1, source_target_pairs={{0,1},{1,2},{2,3},{3,4},{4,5},{5,6},{6,7},{7,0},{8,9},{9,10},{10,1... | collective-permute-start | bytes 307208 | tf_op jit(solution)/shard_map/ppermute | solution.py:12
  416.9 45.9 %copy-start.19 = (f32[128]{0:T(128)S(1)}, f32[128]{0:T(128)}, u32[]{:S(2)}) copy-start(f32[128]{0:T(128)} %copy-done.18) | copy-start | bytes 1540
  417.9 4.7 %collective-permute-start.26 = (f32[1,200,128]{2,1,0:T(8,128)S(1)}, f32[1,200,128]{2,1,0:T(8,128)S(1)}, u32[]{:S(2)}, u32[]{:S(2)}) collective-permute-start(f32[1,200,128]{2,1,0:T(8,128)S(1)} %get-tuple-element.14), channel_id=1, source_target_pairs={{0,24},{8,0},{16,8},{24,16},{1,25},{9,1},{17,9},{25,17},{2,26},{10... | collective-permute-start | bytes 307208 | tf_op jit(solution)/shard_map/ppermute | solution.py:12
  419.7 3.0 collective-permute-start.27
  (6 other events, 30.9 us)
where the time goes:
time: 465 us; the launch traced here: 463 us
  blocking collectives  318 us (68%)
  waiting for transfers between devices  58.1 us (12%)
  matrix products  24.5 us (5%)
  starting transfers between devices  24.4 us (5%)
  other arithmetic  20.7 us (4%)
  local copies, waits for them, and re-layouts  16.7 us (4%)
    psum x3, blocking collectives, energy_total(): return lax.psum(partial_value, ('gx', 'gy'))  117 us
    all_gather x2, blocking collectives, local(): gathered = lax.all_gather(owned, ('gx', 'gy'), axis=0, tiled=True)  80 us
    ppermute x28, waiting for transfers between devices, passed_along(): lax.ppermute(array, axis, [(i, (i + by) % peers) for i in range(peers)])  58.1 us
    all_gather x1, blocking collectives, local(): lax.all_gather(coarse_inverse, ('gx', 'gy'), axis=0, tiled=True)  41.3 us
    unnamed x1, blocking collectives  40.4 us
    psum x1, blocking collectives, local(): curvature = lax.psum(inner_product(direction, product_field), ('gx', 'gy'))  38.5 us
    ppermute x28, starting transfers between devices, passed_along(): lax.ppermute(array, axis, [(i, (i + by) % peers) for i in range(peers)])  24.4 us
  transfers between devices with their start and end apart: 28, of which 20 were waited for; matrix products, arithmetic and copies ran while one was open for 4% of the time, Pallas kernels for 0%

commit v1 on v0

--- a/solution.py
+++ b/solution.py
@@ -71,7 +71,7 @@
         return jnp.sum(left * right, axis=(0, 1, 2))
 
     def energy_total(partial_value):
-        return lax.psum(partial_value, ("gx", "gy"))
+        return jnp.sum(lax.all_gather(partial_value, ("gx", "gy")), axis=0)
 
     residual = rhs[0, 0] * active
     multipliers = jnp.zeros_like(residual)

time: 465 us -> 504 us (1.084)
  blocking collectives: 318 us -> 357 us
    all_gather x0 -> x3, blocking collectives: none -> 119 us  [energy_total(): return jnp.sum(lax.all_gather(partial_value, ('gx', 'gy')), axis=0)]
    psum x3 -> x0, blocking collectives: 117 us -> none  [energy_total(): return lax.psum(partial_value, ('gx', 'gy'))]
    psum x1 -> x2, blocking collectives: 38.5 us -> 76.8 us  [local(): curvature = lax.psum(inner_product(direction, product_field), ('gx', 'gy'))]
  transfers between devices with their start and end apart: 28 -> 28, of which waited for: 20 -> 18; matrix products, arithmetic and copies ran while one was open for 4% -> 4% of each run, Pallas kernels for 0% -> 0%
where the time goes in v1:
time: 504 us; the launch traced here: 503 us
  blocking collectives  357 us (71%)
  waiting for transfers between devices  62.3 us (12%)
  matrix products  23.9 us (5%)
  other arithmetic  21.5 us (4%)
  starting transfers between devices  20 us (4%)
  local copies, waits for them, and re-layouts  16.6 us (3%)
    all_gather x3, blocking collectives, energy_total(): return jnp.sum(lax.all_gather(partial_value, ('gx', 'gy')), axis=0)  119 us
    all_gather x2, blocking collectives, local(): gathered = lax.all_gather(owned, ('gx', 'gy'), axis=0, tiled=True)  80 us
    psum x2, blocking collectives, local(): curvature = lax.psum(inner_product(direction, product_field), ('gx', 'gy'))  76.8 us
    ppermute x28, waiting for transfers between devices, passed_along(): lax.ppermute(array, axis, [(i, (i + by) % peers) for i in range(peers)])  62.3 us
    all_gather x1, blocking collectives, local(): lax.all_gather(coarse_inverse, ('gx', 'gy'), axis=0, tiled=True)  41.3 us
    unnamed x1, blocking collectives  40.4 us
    ppermute x28, starting transfers between devices, passed_along(): lax.ppermute(array, axis, [(i, (i + by) % peers) for i in range(peers)])  20 us
  transfers between devices with their start and end apart: 28, of which 18 were waited for; matrix products, arithmetic and copies ran while one was open for 4% of the time, Pallas kernels for 0%

profile of v1, /device:TPU:0, one launch (start us, length us, event | category | flops | bytes accessed | tf_op | source)
XLA Modules:
  0.0 503.2 jit_solution(6409442317466892802)
XLA Ops:
  1.5 1.9 convolution_bitcast_fusion.4
  4.6 2.6 collective-permute-start
  7.1 1.3 fusion.99
  8.4 1.3 broadcast_multiply_fusion.1
  10.0 1.8 fusion.32
  11.7 1.4 fusion.96
  13.1 40.4 %all-reduce.4 = s32[64]{0:T(128)S(1)} all-reduce(s32[64]{0:T(128)S(1)} %fusion.96), channel_id=1, replica_groups=mesh['gx'=4,'gy'=8] {'gx','gy'}, use_global_device_ids=true, to_apply=%add.4 | all-reduce | flops 64 | bytes 512
  53.8 41.3 %all-gather.4 = f32[32,6,192]{2,1,0:T(8,128)S(1)} all-gather(f32[1,6,192]{2,1,0:T(8,128)} %bitcast.320), channel_id=1, replica_groups=mesh['gx'=4,'gy'=8] {'gx','gy'}, dimensions={0}, use_global_device_ids=true | all-gather | bytes 152064 | tf_op jit(solution)/shard_map/all_gather | solution.py:36
  103.4 2.8 fusion
  106.5 5.0 %collective-permute-done.2 = f32[1,200,128]{2,1,0:T(8,128)S(1)} collective-permute-done((f32[1,200,128]{2,1,0:T(8,128)S(1)}, f32[1,200,128]{2,1,0:T(8,128)S(1)}, u32[]{:S(2)}, u32[]{:S(2)}) %collective-permute-start.2) | collective-permute-done | bytes 102432 | tf_op jit(solution)/shard_map/ppermute | solution.py:12
  113.9 5.6 %collective-permute-done.4 = f32[1,200,128]{2,1,0:T(8,128)S(1)} collective-permute-done((f32[1,200,128]{2,1,0:T(8,128)S(1)}, f32[1,200,128]{2,1,0:T(8,128)S(1)}, u32[]{:S(2)}, u32[]{:S(2)}) %collective-permute-start.4) | collective-permute-done | bytes 102432 | tf_op jit(solution)/shard_map/ppermute | solution.py:12
  121.4 4.8 collective-permute-done.6
  127.7 1.3 gather_fusion.1
  129.0 2.1 collective-permute-done.7
  131.8 39.4 %all-gather.5 = f32[32,6,128]{2,1,0:T(8,128)} all-gather(f32[1,6,128]{2,1,0:T(8,128)S(1)} %reshape.821), channel_id=1, replica_groups=mesh['gx'=4,'gy'=8] {'gx','gy'}, dimensions={0}, use_global_device_ids=true | all-gather | bytes 101376 | tf_op jit(solution)/shard_map/all_gather | solution.py:101
  173.4 3.6 collective-permute-done.8
  177.8 1.9 convert_element_type.109
  182.2 2.0 fusion.7
  184.2 3.2 collective-permute-start.10
  187.4 2.0 collective-permute-start.11
  190.0 1.6 collective-permute-done.11
  191.6 1.3 multiply_reduce_fusion.2
  192.8 38.4 %psum.14 = f32[128]{0:T(128)S(1)} all-reduce(f32[128]{0:T(128)S(1)} %get-tuple-element.2), channel_id=1, replica_groups=mesh['gx'=4,'gy'=8] {'gx','gy'}, use_global_device_ids=true, to_apply=%region_3.4 | all-reduce | flops 128 | bytes 1024 | tf_op jit(solution)/shard_map/psum | solution.py:121
  231.2 39.9 %all-gather.3 = f32[32,1,128]{2,1,0:T(1,128)S(1)} all-gather(f32[1,1,128]{2,1,0:T(1,128)S(1)} %bitcast.326), channel_id=2, replica_groups=mesh['gx'=4,'gy'=8] {'gx','gy'}, dimensions={0}, use_global_device_ids=true | all-gather | bytes 16896 | tf_op jit(solution)/shard_map/all_gather | solution.py:74
  271.7 1.5 multiply_bitcast_fusion.2
  274.8 6.3 %collective-permute-done.12 = f32[1,200,128]{2,1,0:T(8,128)S(1)} collective-permute-done((f32[1,200,128]{2,1,0:T(8,128)S(1)}, f32[1,200,128]{2,1,0:T(8,128)S(1)}, u32[]{:S(2)}, u32[]{:S(2)}) %collective-permute-start.12) | collective-permute-done | bytes 102432 | tf_op jit(solution)/shard_map/ppermute | solution.py:12
  282.3 1.9 collective-permute-start.14
  284.2 2.8 collective-permute-done.14
  288.3 37.8 %all-gather.6 = f32[32,1,128]{2,1,0:T(1,128)} all-gather(f32[1,1,128]{2,1,0:T(1,128)S(1)} %bitcast.328), channel_id=3, replica_groups=mesh['gx'=4,'gy'=8] {'gx','gy'}, dimensions={0}, use_global_device_ids=true | all-gather | bytes 16896 | tf_op jit(solution)/shard_map/all_gather | solution.py:74
  329.3 6.5 %collective-permute-done.16 = f32[1,200,128]{2,1,0:T(8,128)S(1)} collective-permute-done((f32[1,200,128]{2,1,0:T(8,128)S(1)}, f32[1,200,128]{2,1,0:T(8,128)S(1)}, u32[]{:S(2)}, u32[]{:S(2)}) %collective-permute-start.16) | collective-permute-done | bytes 102432 | tf_op jit(solution)/shard_map/ppermute | solution.py:12
  337.2 5.4 %collective-permute-done.18 = f32[2,2,3,128]{3,2,1,0:T(4,128)S(1)} collective-permute-done((f32[2,2,3,128]{3,2,1,0:T(4,128)S(1)}, f32[2,2,3,128]{3,2,1,0:T(4,128)S(1)}, u32[]{:S(2)}, u32[]{:S(2)}) %collective-permute-start.18) | collective-permute-done | bytes 6176 | tf_op jit(solution)/shard_map/ppermute | solution.py:12
  342.7 3.9 collective-permute-done.19
  346.6 40.7 %all-gather.7 = f32[32,6,128]{2,1,0:T(8,128)} all-gather(f32[1,6,128]{2,1,0:T(8,128)S(1)} %reshape.825), channel_id=1, replica_groups=mesh['gx'=4,'gy'=8] {'gx','gy'}, dimensions={0}, use_global_device_ids=true | all-gather | bytes 101376 | tf_op jit(solution)/shard_map/all_gather | solution.py:101
  387.3 1.6 reshape.826
  390.2 3.6 collective-permute-done.20
  393.8 1.8 convert_element_type.113
  395.7 1.4 fusion.64
  397.1 1.9 fusion.6
  399.1 1.9 collective-permute-start.22
  401.0 1.9 collective-permute-start.23
  402.8 1.6 collective-permute-done.22
  406.3 38.4 %psum.15 = f32[128]{0:T(128)S(1)} all-reduce(f32[128]{0:T(128)S(1)} %get-tuple-element.65), channel_id=1, replica_groups=mesh['gx'=4,'gy'=8] {'gx','gy'}, use_global_device_ids=true, to_apply=%region_7.8 | all-reduce | flops 128 | bytes 1024 | tf_op jit(solution)/shard_map/psum | solution.py:121
  444.8 2.1 multiply_bitcast_fusion
  447.8 2.2 collective-permute-start.24
  450.0 4.3 collective-permute-done.24
  456.1 1.8 collective-permute-start.26
  457.9 3.0 collective-permute-done.26
  461.4 41.2 %all-gather.8 = f32[32,1,128]{2,1,0:T(1,128)S(1)} all-gather(f32[1,1,128]{2,1,0:T(1,128)S(1)} %bitcast.327), channel_id=4, replica_groups=mesh['gx'=4,'gy'=8] {'gx','gy'}, dimensions={0}, use_global_device_ids=true | all-gather | bytes 16896 | tf_op jit(solution)/shard_map/all_gather | solution.py:74
  (203 shorter events, 39.6 us)
Async XLA Ops:
  0.6 181.5 %copy-start = (bf16[1,1,1,1200,1200]{4,3,2,1,0:T(8,128)(2,1)S(1)}, bf16[1,1,1,1200,1200]{4,3,2,1,0:T(8,128)(2,1)}, u32[]{:S(2)}) copy-start(bf16[1,1,1,1200,1200]{4,3,2,1,0:T(8,128)(2,1)} %param.8) | copy-start | bytes 8640004
  0.7 110.9 %copy-start.12 = (f32[3]{0:T(128)}, f32[3]{0:T(128)S(1)}, u32[]{:S(2)}) copy-start(f32[3]{0:T(128)S(1)} %compare_select_fusion.4) | copy-start | bytes 40
  4.1 96.6 %collective-permute-start.1 = (f32[1,200,128]{2,1,0:T(8,128)S(1)}, f32[1,200,128]{2,1,0:T(8,128)}, u32[]{:S(2)}, u32[]{:S(2)}) collective-permute-start(f32[1,200,128]{2,1,0:T(8,128)S(1)} %get-tuple-element.45), channel_id=1, source_target_pairs={{0,1},{1,2},{2,3},{3,4},{4,5},{5,6},{6,7},{7,0},{8,9},{9,10},{10,1... | collective-permute-start | bytes 307208 | tf_op jit(solution)/shard_map/ppermute | solution.py:12
  4.6 94.3 %collective-permute-start = (f32[1,200,128]{2,1,0:T(8,128)}, f32[1,200,128]{2,1,0:T(8,128)}, u32[]{:S(2)}, u32[]{:S(2)}) collective-permute-start(f32[1,200,128]{2,1,0:T(8,128)} %get-tuple-element.46), channel_id=1, source_target_pairs={{0,8},{8,16},{16,24},{24,0},{1,9},{9,17},{17,25},{25,1},{2,10},{10... | collective-permute-start | bytes 307208 | tf_op jit(solution)/shard_map/ppermute | solution.py:12
  98.8 12.7 %copy-start.22 = (f32[3]{0:T(128)}, f32[3]{0:T(128)S(1)}, u32[]{:S(2)}) copy-start(f32[3]{0:T(128)S(1)} %pad.44.clone) | copy-start | bytes 40
  106.3 14.1 %copy-start.11 = (bf16[1,1,1,24,1200]{4,3,2,1,0:T(8,128)(2,1)S(1)}, bf16[1,1,1,24,1200]{4,3,2,1,0:T(8,128)(2,1)}, u32[]{:S(2)}) copy-start(bf16[1,1,1,24,1200]{4,3,2,1,0:T(8,128)(2,1)} %param.10) | copy-start | bytes 172804
  106.3 20.6 %copy-start.16 = (s32[192,1]{0,1:T(1,128)S(1)}, s32[192,1]{0,1:T(1,128)}, u32[]{:S(2)}) copy-start(s32[192,1]{0,1:T(1,128)} %compare_select_fusion) | copy-start | bytes 2308
  106.3 5.2 %collective-permute-start.2 = (f32[1,200,128]{2,1,0:T(8,128)S(1)}, f32[1,200,128]{2,1,0:T(8,128)S(1)}, u32[]{:S(2)}, u32[]{:S(2)}) collective-permute-start(f32[1,200,128]{2,1,0:T(8,128)S(1)} %get-tuple-element.32), channel_id=1, source_target_pairs={{0,24},{8,0},{16,8},{24,16},{1,25},{9,1},{17,9},{25,17},{2,26},{10... | collective-permute-start | bytes 307208 | tf_op jit(solution)/shard_map/ppermute | solution.py:12
  106.4 5.1 %collective-permute-start.3 = (f32[1,200,128]{2,1,0:T(8,128)S(1)}, f32[1,200,128]{2,1,0:T(8,128)S(1)}, u32[]{:S(2)}, u32[]{:S(2)}) collective-permute-start(f32[1,200,128]{2,1,0:T(8,128)S(1)} %get-tuple-element.33), channel_id=1, source_target_pairs={{0,7},{1,0},{2,1},{3,2},{4,3},{5,4},{6,5},{7,6},{8,15},{9,8},{10,9... | collective-permute-start | bytes 307208 | tf_op jit(solution)/shard_map/ppermute | solution.py:12
  112.9 6.5 %collective-permute-start.4 = (f32[1,200,128]{2,1,0:T(8,128)S(1)}, f32[1,200,128]{2,1,0:T(8,128)S(1)}, u32[]{:S(2)}, u32[]{:S(2)}) collective-permute-start(f32[1,200,128]{2,1,0:T(8,128)S(1)} %get-tuple-element.44), channel_id=1, source_target_pairs={{0,8},{8,16},{16,24},{24,0},{1,9},{9,17},{17,25},{25,1},{2,10},{10... | collective-permute-start | bytes 307208 | tf_op jit(solution)/shard_map/ppermute | solution.py:12
  113.1 6.4 %collective-permute-start.5 = (f32[1,200,128]{2,1,0:T(8,128)S(1)}, f32[1,200,128]{2,1,0:T(8,128)S(1)}, u32[]{:S(2)}, u32[]{:S(2)}) collective-permute-start(f32[1,200,128]{2,1,0:T(8,128)S(1)} %get-tuple-element.43), channel_id=1, source_target_pairs={{0,1},{1,2},{2,3},{3,4},{4,5},{5,6},{6,7},{7,0},{8,9},{9,10},{10,1... | collective-permute-start | bytes 307208 | tf_op jit(solution)/shard_map/ppermute | solution.py:12
  120.8 5.5 %collective-permute-start.6 = (f32[2,2,3,128]{3,2,1,0:T(4,128)S(1)}, f32[2,2,3,128]{3,2,1,0:T(4,128)S(1)}, u32[]{:S(2)}, u32[]{:S(2)}) collective-permute-start(f32[2,2,3,128]{3,2,1,0:T(4,128)S(1)} %fusion.85), channel_id=1, source_target_pairs={{0,8},{8,16},{16,24},{24,0},{1,9},{9,17},{17,25},{25,1},{2,10},{10... | collective-permute-start | bytes 18440 | tf_op jit(solution)/shard_map/ppermute | solution.py:12
  126.9 4.2 collective-permute-start.7
  173.3 3.7 collective-permute-start.8
  177.6 2.0 collective-permute-start.9
  181.7 9.9 %copy-start.5 = (f32[1,1,1,3,200,128]{5,4,3,2,1,0:T(8,128)S(1)}, f32[1,1,1,3,200,128]{5,4,3,2,1,0:T(8,128)}, u32[]{:S(2)}) copy-start(f32[1,1,1,3,200,128]{5,4,3,2,1,0:T(8,128)} %param.7) | copy-start | bytes 921604
  181.7 9.9 %copy-start.13 = (f32[3]{0:T(128)S(1)}, f32[3]{0:T(128)}, u32[]{:S(2)}) copy-start(f32[3]{0:T(128)} %copy-done.12) | copy-start | bytes 40
  181.7 9.9 %copy-start.23 = (f32[3]{0:T(128)S(1)}, f32[3]{0:T(128)}, u32[]{:S(2)}) copy-start(f32[3]{0:T(128)} %copy-done.22) | copy-start | bytes 40
  182.2 89.6 %copy-start.14 = (f32[3]{0:T(128)S(1)}, f32[3]{0:T(128)}, u32[]{:S(2)}) copy-start(f32[3]{0:T(128)} %copy-done.12) | copy-start | bytes 40
  184.2 5.8 %collective-permute-start.10 = (f32[1,200,128]{2,1,0:T(8,128)S(1)}, f32[1,200,128]{2,1,0:T(8,128)S(1)}, u32[]{:S(2)}, u32[]{:S(2)}) collective-permute-start(f32[1,200,128]{2,1,0:T(8,128)S(1)} %get-tuple-element.27), channel_id=1, source_target_pairs={{0,24},{8,0},{16,8},{24,16},{1,25},{9,1},{17,9},{25,17},{2,26},{10... | collective-permute-start | bytes 307208 | tf_op jit(solution)/shard_map/ppermute | solution.py:12
  187.4 4.2 collective-permute-start.11
  271.1 55.7 %copy-start.18 = (f32[128]{0:T(128)}, f32[128]{0:T(128)S(1)}, u32[]{:S(2)}) copy-start(f32[128]{0:T(128)S(1)} %reduce_sum.73) | copy-start | bytes 1540
  271.1 10.1 %copy-start.1 = (bf16[1,1,1,1200,1200]{4,3,2,1,0:T(8,128)(2,1)S(1)}, bf16[1,1,1,1200,1200]{4,3,2,1,0:T(8,128)(2,1)}, u32[]{:S(2)}) copy-start(bf16[1,1,1,1200,1200]{4,3,2,1,0:T(8,128)(2,1)} %param.9) | copy-start | bytes 8640004
  273.2 13.8 %copy-start.6 = (f32[3,200,128]{2,1,0:T(8,128)}, f32[3,200,128]{2,1,0:T(8,128)S(1)}, u32[]{:S(2)}) copy-start(f32[3,200,128]{2,1,0:T(8,128)S(1)} %get-tuple-element.11) | copy-start | bytes 921604
  274.1 7.0 %collective-permute-start.12 = (f32[1,200,128]{2,1,0:T(8,128)S(1)}, f32[1,200,128]{2,1,0:T(8,128)S(1)}, u32[]{:S(2)}, u32[]{:S(2)}) collective-permute-start(f32[1,200,128]{2,1,0:T(8,128)S(1)} %get-tuple-element.42), channel_id=1, source_target_pairs={{0,8},{8,16},{16,24},{24,0},{1,9},{9,17},{17,25},{25,1},{2,10},{10... | collective-permute-start | bytes 307208 | tf_op jit(solution)/shard_map/ppermute | solution.py:12
  274.2 6.9 %collective-permute-start.13 = (f32[1,200,128]{2,1,0:T(8,128)S(1)}, f32[1,200,128]{2,1,0:T(8,128)S(1)}, u32[]{:S(2)}, u32[]{:S(2)}) collective-permute-start(f32[1,200,128]{2,1,0:T(8,128)S(1)} %get-tuple-element.41), channel_id=1, source_target_pairs={{0,1},{1,2},{2,3},{3,4},{4,5},{5,6},{6,7},{7,0},{8,9},{9,10},{10,1... | collective-permute-start | bytes 307208 | tf_op jit(solution)/shard_map/ppermute | solution.py:12
  282.3 106.5 %copy-start.9 = (f32[192,6]{1,0:T(8,128)S(1)}, f32[192,6]{1,0:T(8,128)}, u32[]{:S(2)}) copy-start(f32[192,6]{1,0:T(8,128)} %gather_fusion.1) | copy-start | bytes 13828
  282.3 4.7 collective-permute-start.14
  284.2 2.8 collective-permute-start.15
  328.9 7.0 %collective-permute-start.16 = (f32[1,200,128]{2,1,0:T(8,128)S(1)}, f32[1,200,128]{2,1,0:T(8,128)S(1)}, u32[]{:S(2)}, u32[]{:S(2)}) collective-permute-start(f32[1,200,128]{2,1,0:T(8,128)S(1)} %get-tuple-element.40), channel_id=1, source_target_pairs={{0,8},{8,16},{16,24},{24,0},{1,9},{9,17},{17,25},{25,1},{2,10},{10... | collective-permute-start | bytes 307208 | tf_op jit(solution)/shard_map/ppermute | solution.py:12
  329.0 6.9 %collective-permute-start.17 = (f32[1,200,128]{2,1,0:T(8,128)S(1)}, f32[1,200,128]{2,1,0:T(8,128)S(1)}, u32[]{:S(2)}, u32[]{:S(2)}) collective-permute-start(f32[1,200,128]{2,1,0:T(8,128)S(1)} %get-tuple-element.39), channel_id=1, source_target_pairs={{0,1},{1,2},{2,3},{3,4},{4,5},{5,6},{6,7},{7,0},{8,9},{9,10},{10,1... | collective-permute-start | bytes 307208 | tf_op jit(solution)/shard_map/ppermute | solution.py:12
  337.2 5.5 %collective-permute-start.18 = (f32[2,2,3,128]{3,2,1,0:T(4,128)S(1)}, f32[2,2,3,128]{3,2,1,0:T(4,128)S(1)}, u32[]{:S(2)}, u32[]{:S(2)}) collective-permute-start(f32[2,2,3,128]{3,2,1,0:T(4,128)S(1)} %fusion.83), channel_id=1, source_target_pairs={{0,8},{8,16},{16,24},{24,0},{1,9},{9,17},{17,25},{25,1},{2,10},{10... | collective-permute-start | bytes 18440 | tf_op jit(solution)/shard_map/ppermute | solution.py:12
  342.7 3.9 collective-permute-start.19
  390.1 3.7 collective-permute-start.20
  393.8 1.8 collective-permute-start.21
  395.6 9.4 %copy-start.8 = (f32[3,200,128]{2,1,0:T(8,128)S(1)}, f32[3,200,128]{2,1,0:T(8,128)}, u32[]{:S(2)}) copy-start(f32[3,200,128]{2,1,0:T(8,128)} %copy-done.7) | copy-start | bytes 921604
  395.6 9.4 %copy-start.15 = (f32[3]{0:T(128)S(1)}, f32[3]{0:T(128)}, u32[]{:S(2)}) copy-start(f32[3]{0:T(128)} %copy-done.12) | copy-start | bytes 40
  395.7 9.4 %copy-start.25 = (f32[3]{0:T(128)S(1)}, f32[3]{0:T(128)}, u32[]{:S(2)}) copy-start(f32[3]{0:T(128)} %copy-done.22) | copy-start | bytes 40
  397.1 47.7 %copy-start.21 = (f32[128]{0:T(128)S(1)}, f32[128]{0:T(128)}, u32[]{:S(2)}) copy-start(f32[128]{0:T(128)} %copy-done.20) | copy-start | bytes 1540
  397.1 47.7 %copy-start.17 = (f32[128]{0:T(128)S(1)}, f32[128]{0:T(128)}, u32[]{:S(2)}) copy-start(f32[128]{0:T(128)} %get-tuple-element.6) | copy-start | bytes 1540
  399.1 5.3 %collective-permute-start.22 = (f32[1,200,128]{2,1,0:T(8,128)S(1)}, f32[1,200,128]{2,1,0:T(8,128)S(1)}, u32[]{:S(2)}, u32[]{:S(2)}) collective-permute-start(f32[1,200,128]{2,1,0:T(8,128)S(1)} %get-tuple-element.17), channel_id=1, source_target_pairs={{0,24},{8,0},{16,8},{24,16},{1,25},{9,1},{17,9},{25,17},{2,26},{10... | collective-permute-start | bytes 307208 | tf_op jit(solution)/shard_map/ppermute | solution.py:12
  401.0 4.1 collective-permute-start.23
  444.8 10.3 %copy-start.2 = (bf16[1,1,1,1200,1200]{4,3,2,1,0:T(8,128)(2,1)S(1)}, bf16[1,1,1,1200,1200]{4,3,2,1,0:T(8,128)(2,1)}, u32[]{:S(2)}) copy-start(bf16[1,1,1,1200,1200]{4,3,2,1,0:T(8,128)(2,1)} %param.9) | copy-start | bytes 8640004
  447.8 6.5 %collective-permute-start.24 = (f32[1,200,128]{2,1,0:T(8,128)S(1)}, f32[1,200,128]{2,1,0:T(8,128)S(1)}, u32[]{:S(2)}, u32[]{:S(2)}) collective-permute-start(f32[1,200,128]{2,1,0:T(8,128)S(1)} %get-tuple-element.38), channel_id=1, source_target_pairs={{0,8},{8,16},{16,24},{24,0},{1,9},{9,17},{17,25},{25,1},{2,10},{10... | collective-permute-start | bytes 307208 | tf_op jit(solution)/shard_map/ppermute | solution.py:12
  450.0 5.0 collective-permute-start.25
  455.1 47.6 %copy-start.19 = (f32[128]{0:T(128)S(1)}, f32[128]{0:T(128)}, u32[]{:S(2)}) copy-start(f32[128]{0:T(128)} %copy-done.18) | copy-start | bytes 1540
  456.1 4.7 collective-permute-start.26
  457.9 3.0 collective-permute-start.27
  (6 other events, 30.9 us)
